TPU v7x, 32 devices: a whole 2x2x4 slice. The times are simulated.
32 devices in a mesh: wide: 16 (over z, y, x), narrow: 2 (over core).
Axes of the slice: x: 2, y: 2, z: 4, core: 2. Of those that a mesh axis runs over, the one named last changes fastest.
Arguments:
- tokens: bfloat16 [32, 200, 768], P(('wide', 'narrow')), may hold values from -6 to 6
- memory_raw: bfloat16 [32, 896, 768], P(('wide', 'narrow')), may hold values from -22 to 22
- lengths: int32 [32], P(('wide', 'narrow')), may hold values from 5 to 200, as said below
- cotangent: bfloat16 [32, 200, 768], P(('wide', 'narrow')), may hold values from -6 to 6
- self_proj: bfloat16 [4, 768, 768], P(None, ('wide', 'narrow')), may hold values from -0.21875 to 0.21875
- cross_proj: bfloat16 [4, 768, 768], P(None, ('wide', 'narrow')), may hold values from -0.21875 to 0.21875
- ffn_pair: bfloat16 [2, 768, 3072], P(None, ('wide', 'narrow')), may hold values from -0.21875 to 0.21875
- ffn_gain: bfloat16 [3072], P(('wide', 'narrow')), may hold values from 0.5 to 1.5
- norm_gains: bfloat16 [5, 768], P(None, ('wide', 'narrow')), may hold values from 0.5 to 1.5
- rel_table: bfloat16 [512, 12], P(('wide', 'narrow')), may hold values from -5 to 5
- head_gain: bfloat16 [2, 12], replicated, may hold values from 0.099609375 to 1.8984375
- bn_scale: bfloat16 [768], P(('wide', 'narrow')), may hold values from 0.099609375 to 1.8984375
- bn_bias: bfloat16 [768], P(('wide', 'narrow')), may hold values from -3 to 3
Outputs:
- output: bfloat16 [32, 200, 768], P(('wide', 'narrow'))
- d_tokens: float32 [32, 200, 768], P(('wide', 'narrow'))
- d_memory: float32 [32, 896, 768], P(('wide', 'narrow'))
- d_self_proj: float32 [4, 768, 768], P(None, ('wide', 'narrow'))
- d_cross_proj: float32 [4, 768, 768], P(None, ('wide', 'narrow'))
- d_ffn_pair: float32 [2, 768, 3072], P(None, ('wide', 'narrow'))
- d_ffn_gain: float32 [3072], P(('wide', 'narrow'))
- d_norm_gains: float32 [5, 768], P(None, ('wide', 'narrow'))
- d_rel_table: float32 [512, 12], P(('wide', 'narrow'))
- d_head_gain: float32 [2, 12], replicated
- d_bn_scale: float32 [768], P(('wide', 'narrow'))
- d_bn_bias: float32 [768], P(('wide', 'narrow'))
Inputs may be any that keep to these rules, and one draw needn't show every extreme that they name: `lengths`: some item has exactly 200 decoder tokens in every draw.
All inputs are finite; a program needn't handle non-finite values.
Results may differ from a plain program's by a relative error of at most 0.02.
Values may be sent and summed in bfloat16 or wider, within the bound.
A program may use at most 256 MiB of HBM per device.

v0:
```python
from functools import partial
import math
import jax
import jax.numpy as jnp
import numpy as np
from jax import lax
from jax.sharding import PartitionSpec as P

EPSILON = 1e-05
NEGATIVE = -1000000000.0
HIGHEST = lax.Precision.HIGHEST


def bucket_select(length, buckets):
    select = np.zeros((buckets, length), np.float32)
    for distance in range(length):
        if distance <= 128:
            bucket = 255 - distance
        else:
            scaled = math.log(distance / 128.0) / math.log(1023.0 / 128.0) * 127.0
            bucket = 255 - (int(math.ceil(scaled)) + 128)
        select[bucket, distance] = 1.0
    return select


def toeplitz(by_distance):
    head_count, row_count = by_distance.shape
    padded = jnp.concatenate([by_distance[:, ::-1], jnp.zeros_like(by_distance)], axis=1)
    repeated = jnp.tile(padded, (1, row_count))[:, : row_count * (2 * row_count - 1)]
    shaped = repeated.reshape(head_count, row_count, 2 * row_count - 1)
    return shaped[:, :, row_count - 1 :]


def norm_forward(values, gain_row):
    centred = values - jnp.mean(values, axis=-1, keepdims=True)
    variance = jnp.mean(centred * centred, axis=-1, keepdims=True)
    return centred * lax.rsqrt(variance + EPSILON) * gain_row


def norm_backward(values, gain_row, upstream):
    unused, pullback = jax.vjp(norm_forward, values, gain_row)
    return pullback(upstream)


def product(left_side, right_side):
    return jnp.dot(left_side, right_side, preferred_element_type=jnp.float32)


def back_product(upstream, weight):
    return jnp.einsum("ble,de->bld", upstream, weight, preferred_element_type=jnp.float32)


def weight_grad(activation, upstream):
    return jnp.einsum("bld,ble->de", activation, upstream, preferred_element_type=jnp.float32)


def to_heads(values, head_count):
    return values.reshape(
        values.shape[0], values.shape[1], head_count, values.shape[2] // head_count
    )


def from_heads(values):
    return values.reshape(values.shape[0], values.shape[1], values.shape[2] * values.shape[3])


def attend_scores(queries, key_rows, score_bias, allowed, inv_root):
    scores = (
        jnp.einsum("bqhe,bkhe->bhqk", queries, key_rows, preferred_element_type=jnp.float32)
        * inv_root
    )
    if score_bias is None:
        return scores
    return jnp.where(allowed, scores + score_bias, NEGATIVE)


def attend_forward(queries, key_rows, values, score_bias, allowed, head_scale, inv_root):
    scores = attend_scores(queries, key_rows, score_bias, allowed, inv_root)
    maximum = jnp.max(scores, axis=-1, keepdims=True)
    totals = maximum + jnp.log(jnp.sum(jnp.exp(scores - maximum), axis=-1, keepdims=True))
    softmax_low = jnp.exp(scores - totals).astype(jnp.bfloat16)
    attended = jnp.einsum(
        "bhqk,bkhe->bqhe", softmax_low, values, preferred_element_type=jnp.float32
    )
    scaled = (attended * head_scale[:, None]).astype(jnp.bfloat16)
    return (attended, from_heads(scaled), totals)


def attend_backward(
    queries, key_rows, values, score_bias, allowed, head_scale, inv_root, totals, attended, upstream
):
    head_grad = jnp.sum(upstream * attended, axis=(0, 1, 3))
    grad_attended = (upstream * head_scale[:, None]).astype(jnp.bfloat16)
    softmax_out = jnp.exp(attend_scores(queries, key_rows, score_bias, allowed, inv_root) - totals)
    softmax_low = softmax_out.astype(jnp.bfloat16)
    grad_soft = jnp.einsum(
        "bqhe,bkhe->bhqk", grad_attended, values, preferred_element_type=jnp.float32
    )
    grad_values = jnp.einsum(
        "bhqk,bqhe->bkhe", softmax_low, grad_attended, preferred_element_type=jnp.float32
    )
    grad_scores = softmax_out * (
        grad_soft - jnp.sum(softmax_out * grad_soft, axis=-1, keepdims=True)
    )
    grad_scores = grad_scores.astype(jnp.bfloat16)
    grad_queries = (
        jnp.einsum("bhqk,bkhe->bqhe", grad_scores, key_rows, preferred_element_type=jnp.float32)
        * inv_root
    )
    grad_keys = (
        jnp.einsum("bhqk,bqhe->bkhe", grad_scores, queries, preferred_element_type=jnp.float32)
        * inv_root
    )
    return (
        head_grad,
        grad_scores,
        from_heads(grad_queries.astype(jnp.bfloat16)),
        from_heads(grad_keys.astype(jnp.bfloat16)),
        from_heads(grad_values.astype(jnp.bfloat16)),
    )


def body(
    tokens,
    memory_raw,
    lengths,
    cotangent,
    self_proj,
    cross_proj,
    ffn_pair,
    ffn_gain,
    norm_gains,
    rel_table,
    head_gain,
    bn_scale,
    bn_bias,
):
    item_count, length, model_width = tokens.shape
    head_count = head_gain.shape[1]
    inv_root = 1.0 / math.sqrt(model_width // head_count)
    mem_rows = memory_raw.shape[1]
    head_scales = head_gain.astype(jnp.float32)
    self_full, gains_full, table_full = (
        lax.all_gather(self_proj, ("wide", "narrow"), axis=1, tiled=True),
        lax.all_gather(norm_gains, ("wide", "narrow"), axis=1, tiled=True),
        lax.all_gather(rel_table, ("wide", "narrow"), axis=0, tiled=True),
    )
    norm_scale = gains_full.astype(jnp.float32)
    select = jnp.asarray(bucket_select(length, table_full.shape[0]))
    by_distance = jnp.einsum("th,td->hd", table_full.astype(jnp.float32), select, precision=HIGHEST)
    score_bias = toeplitz(by_distance)[None]
    positions = jnp.arange(length)
    causal = positions[None, :] <= positions[:, None]
    live_keys = positions[None, :] < lengths[:, None]
    allowed = causal[None, None] & live_keys[:, None, None, :]
    token_values = tokens.astype(jnp.float32)
    normed_one = norm_forward(token_values, norm_scale[0]).astype(jnp.bfloat16)
    self_queries = to_heads(product(normed_one, self_full[0]).astype(jnp.bfloat16), head_count)
    self_keys = to_heads(product(normed_one, self_full[1]).astype(jnp.bfloat16), head_count)
    self_values = to_heads(product(normed_one, self_full[2]).astype(jnp.bfloat16), head_count)
    self_attended, self_flat, self_totals = attend_forward(
        self_queries, self_keys, self_values, score_bias, allowed, head_scales[0], inv_root
    )
    self_branch = product(self_flat, self_full[3])
    residual_one = token_values + norm_forward(self_branch, norm_scale[1])
    cross_full, scale_full, shift_full = (
        lax.all_gather(cross_proj, ("wide", "narrow"), axis=1, tiled=True),
        lax.all_gather(bn_scale, ("wide", "narrow"), axis=0, tiled=True),
        lax.all_gather(bn_bias, ("wide", "narrow"), axis=0, tiled=True),
    )
    memory_values = memory_raw.astype(jnp.float32)
    plain_sum, square_sum = lax.psum(
        (jnp.sum(memory_values, axis=(0, 1)), jnp.sum(memory_values * memory_values, axis=(0, 1))),
        ("wide", "narrow"),
    )
    row_total = item_count * mem_rows * lax.axis_size(("wide", "narrow"))
    bn_mean = plain_sum / row_total
    inv_std = lax.rsqrt(square_sum / row_total - bn_mean * bn_mean + EPSILON)
    centred_mem = (memory_values - bn_mean) * inv_std
    bn_gain = scale_full.astype(jnp.float32)
    memory_low = (centred_mem * bn_gain + shift_full.astype(jnp.float32)).astype(jnp.bfloat16)
    normed_two = norm_forward(residual_one, norm_scale[2]).astype(jnp.bfloat16)
    cross_queries = to_heads(product(normed_two, cross_full[0]).astype(jnp.bfloat16), head_count)
    cross_keys = to_heads(product(memory_low, cross_full[1]).astype(jnp.bfloat16), head_count)
    cross_values = to_heads(product(memory_low, cross_full[2]).astype(jnp.bfloat16), head_count)
    cross_attended, cross_flat, cross_totals = attend_forward(
        cross_queries, cross_keys, cross_values, None, None, head_scales[1], inv_root
    )
    cross_branch = product(cross_flat, cross_full[3])
    residual_two = residual_one + norm_forward(cross_branch, norm_scale[3])
    ffn_full, ffn_scale = (
        lax.all_gather(ffn_pair, ("wide", "narrow"), axis=1, tiled=True),
        lax.all_gather(ffn_gain, ("wide", "narrow"), axis=0, tiled=True),
    )
    normed_three = norm_forward(residual_two, norm_scale[4]).astype(jnp.bfloat16)
    hidden = product(normed_three, ffn_full[0])
    activated = jax.nn.gelu(hidden, approximate=False)
    unit_scale = ffn_scale.astype(jnp.float32)
    rescaled = norm_forward(activated, unit_scale).astype(jnp.bfloat16)
    ffn_branch = jnp.einsum(
        "blf,df->bld", rescaled, ffn_full[1], preferred_element_type=jnp.float32
    )
    output = (residual_two + ffn_branch).astype(jnp.bfloat16)
    ffn_back = lax.all_gather(ffn_pair, ("wide", "narrow"), axis=1, tiled=True)
    upstream = cotangent.astype(jnp.float32)
    grad_rescaled = jnp.einsum(
        "bld,df->blf", cotangent, ffn_back[1], preferred_element_type=jnp.float32
    )
    grad_activated, grad_unit_scale = norm_backward(activated, unit_scale, grad_rescaled)
    unused, gelu_pull = jax.vjp(partial(jax.nn.gelu, approximate=False), hidden)
    grad_hidden = gelu_pull(grad_activated)[0].astype(jnp.bfloat16)
    grad_normed_three = jnp.einsum(
        "blf,df->bld", grad_hidden, ffn_back[0], preferred_element_type=jnp.float32
    )
    grad_two_part, grad_scale_four = norm_backward(residual_two, norm_scale[4], grad_normed_three)
    grad_res_two = upstream + grad_two_part
    grad_in = weight_grad(normed_three, grad_hidden)
    grad_out = weight_grad(cotangent, rescaled)
    ffn_grad_shard = jnp.transpose(
        lax.psum_scatter(
            jnp.stack([grad_in, grad_out], axis=1),
            ("wide", "narrow"),
            scatter_dimension=0,
            tiled=True,
        ),
        (1, 0, 2),
    )
    cross_back = lax.all_gather(cross_proj, ("wide", "narrow"), axis=1, tiled=True)
    grad_cross_branch, grad_scale_three = norm_backward(cross_branch, norm_scale[3], grad_res_two)
    grad_cross_low = grad_cross_branch.astype(jnp.bfloat16)
    grad_cross_scaled = to_heads(back_product(grad_cross_low, cross_back[3]), head_count)
    cross_head, unused_scores, grad_cross_query, grad_cross_key, grad_cross_value = attend_backward(
        cross_queries,
        cross_keys,
        cross_values,
        None,
        None,
        head_scales[1],
        inv_root,
        cross_totals,
        cross_attended,
        grad_cross_scaled,
    )
    grad_memory = back_product(grad_cross_key, cross_back[1]) + back_product(
        grad_cross_value, cross_back[2]
    )
    grad_one_part, grad_scale_two = norm_backward(
        residual_one, norm_scale[2], back_product(grad_cross_query, cross_back[0])
    )
    grad_res_one = grad_res_two + grad_one_part
    cross_grad_shard = jnp.transpose(
        lax.psum_scatter(
            jnp.stack(
                [
                    weight_grad(normed_two, grad_cross_query),
                    weight_grad(memory_low, grad_cross_key),
                    weight_grad(memory_low, grad_cross_value),
                    weight_grad(cross_flat, grad_cross_low),
                ],
                axis=1,
            ),
            ("wide", "narrow"),
            scatter_dimension=0,
            tiled=True,
        ),
        (1, 0, 2),
    )
    self_back = lax.all_gather(self_proj, ("wide", "narrow"), axis=1, tiled=True)
    grad_self_branch, grad_scale_one = norm_backward(self_branch, norm_scale[1], grad_res_one)
    grad_self_low = grad_self_branch.astype(jnp.bfloat16)
    grad_self_scaled = to_heads(back_product(grad_self_low, self_back[3]), head_count)
    self_head, grad_bias_scores, grad_self_query, grad_self_key, grad_self_value = attend_backward(
        self_queries,
        self_keys,
        self_values,
        score_bias,
        allowed,
        head_scales[0],
        inv_root,
        self_totals,
        self_attended,
        grad_self_scaled,
    )
    grad_bias = jnp.sum(grad_bias_scores.astype(jnp.float32), axis=0)
    unused_value, toeplitz_pull = jax.vjp(toeplitz, by_distance)
    grad_distance = toeplitz_pull(grad_bias)[0]
    grad_table = jnp.einsum("td,hd->th", select, grad_distance, precision=HIGHEST)
    grad_normed_one = (
        back_product(grad_self_query, self_back[0])
        + back_product(grad_self_key, self_back[1])
        + back_product(grad_self_value, self_back[2])
    )
    grad_tokens_part, grad_scale_zero = norm_backward(token_values, norm_scale[0], grad_normed_one)
    grad_tokens = grad_res_one + grad_tokens_part
    gain_grads = jnp.stack(
        [grad_scale_zero, grad_scale_one, grad_scale_two, grad_scale_three, grad_scale_four]
    )
    self_grad_shard = jnp.transpose(
        lax.psum_scatter(
            jnp.stack(
                [
                    weight_grad(normed_one, grad_self_query),
                    weight_grad(normed_one, grad_self_key),
                    weight_grad(normed_one, grad_self_value),
                    weight_grad(self_flat, grad_self_low),
                ],
                axis=1,
            ),
            ("wide", "narrow"),
            scatter_dimension=0,
            tiled=True,
        ),
        (1, 0, 2),
    )
    bias_part = jnp.sum(grad_memory, axis=(0, 1))
    scale_part = jnp.sum(grad_memory * centred_mem, axis=(0, 1))
    bn_totals, head_totals, gain_totals, table_totals, unit_totals = lax.psum(
        (
            jnp.stack([scale_part, bias_part]),
            jnp.stack([self_head, cross_head]),
            gain_grads,
            grad_table,
            grad_unit_scale,
        ),
        ("wide", "narrow"),
    )
    grad_memory_raw = (
        bn_gain
        * inv_std
        * (grad_memory - bn_totals[1] / row_total - centred_mem * (bn_totals[0] / row_total))
    )
    position = lax.axis_index(("wide", "narrow"))
    shard_width = bn_scale.shape[0]
    offset = position * shard_width
    bn_scale_shard = lax.dynamic_slice_in_dim(bn_totals[0], offset, shard_width)
    bn_bias_shard = lax.dynamic_slice_in_dim(bn_totals[1], offset, shard_width)
    gain_shard = lax.dynamic_slice_in_dim(gain_totals, offset, shard_width, 1)
    table_rows = rel_table.shape[0]
    table_shard = lax.dynamic_slice_in_dim(table_totals, position * table_rows, table_rows, 0)
    unit_width = ffn_gain.shape[0]
    ffn_gain_shard = lax.dynamic_slice_in_dim(unit_totals, position * unit_width, unit_width)
    return (
        output,
        grad_tokens,
        grad_memory_raw,
        self_grad_shard,
        cross_grad_shard,
        ffn_grad_shard,
        ffn_gain_shard,
        gain_shard,
        table_shard,
        head_totals,
        bn_scale_shard,
        bn_bias_shard,
    )


def solution(mesh):
    return jax.shard_map(
        body,
        mesh=mesh,
        in_specs=(
            P(("wide", "narrow"), None, None),
            P(("wide", "narrow"), None, None),
            P(("wide", "narrow")),
            P(("wide", "narrow"), None, None),
            P(None, ("wide", "narrow"), None),
            P(None, ("wide", "narrow"), None),
            P(None, ("wide", "narrow"), None),
            P(("wide", "narrow")),
            P(None, ("wide", "narrow")),
            P(("wide", "narrow"), None),
            P(),
            P(("wide", "narrow")),
            P(("wide", "narrow")),
        ),
        out_specs=(
            P(("wide", "narrow"), None, None),
            P(("wide", "narrow"), None, None),
            P(("wide", "narrow"), None, None),
            P(None, ("wide", "narrow"), None),
            P(None, ("wide", "narrow"), None),
            P(None, ("wide", "narrow"), None),
            P(("wide", "narrow")),
            P(None, ("wide", "narrow")),
            P(("wide", "narrow"), None),
            P(),
            P(("wide", "narrow")),
            P(("wide", "narrow")),
        ),
        check_vma=False,
    )
```

profile of v0, /device:TPU:0, one launch (start us, length us, event | category | flops | bytes accessed | tf_op | source)
XLA Modules:
  0.0 789.1 jit_solution(18137950825026918576)
XLA Ops:
  13.3 42.3 %all-reduce.8 = (bf16[768]{0:T(1024)(128)(2,1)S(1)}, bf16[768]{0:T(1024)(128)(2,1)S(1)}, bf16[3072]{0:T(1024)(128)(2,1)S(1)}) all-reduce(bf16[768]{0:T(1024)(128)(2,1)S(1)} %dynamic-update-slice.1, bf16[768]{0:T(1024)(128)(2,1)S(1)} %dynamic-update-slice, ...), channel_id=1, replica_groups=mesh['wide'=16,'narrow'=2] {'wide','narrow'}, use_global_device_ids=true, to_apply=%add.4 | all-reduce | flops 4608 | bytes 18432
  57.4 40.9 %all-gather = bf16[32,24,5]{1,2,0:T(8,128)(2,1)S(1)} all-gather(bf16[1,24,5]{1,2,0:T(8,128)(2,1)} %bitcast.348), channel_id=1, replica_groups=mesh['wide'=16,'narrow'=2] {'wide','narrow'}, dimensions={0}, use_global_device_ids=true | all-gather | bytes 7920 | tf_op jit(solution)/shard_map/all_gather | solution.py:145
  98.6 37.8 %all_gather.29 = bf16[512,12]{1,0:T(8,128)(2,1)S(1)} all-gather(bf16[16,12]{1,0:T(8,128)(2,1)} %param.23), channel_id=1, replica_groups=mesh['wide'=16,'narrow'=2] {'wide','narrow'}, dimensions={0}, use_global_device_ids=true | all-gather | bytes 12672 | tf_op jit(solution)/shard_map/all_gather | solution.py:146
  138.0 2.9 tile.4
  140.9 7.0 tile.10
  147.9 5.1 slice.107
  153.0 7.2 reshape.913
  160.2 4.2 slice.108
  164.4 3.4 copy.99
  168.2 39.5 %all-reduce.7 = (f32[768]{0:T(1024)S(1)}, f32[768]{0:T(1024)S(1)}) all-reduce(f32[768]{0:T(1024)S(1)} %get-tuple-element.19, f32[768]{0:T(1024)S(1)} %get-tuple-element.18), channel_id=1, replica_groups=mesh['wide'=16,'narrow'=2] {'wide','narrow'}, use_global_device_ids=true, to_apply=%region_9.10 | all-reduce | flops 1536 | bytes 12288 | tf_op jit(solution)/shard_map/psum | solution.py:172
  210.6 1.8 convolution_convert_fusion.6
  212.6 1.9 convolution_convert_fusion.5
  215.4 1.8 convolution_convert_fusion.7
  217.3 2.6 fusion.107
  220.6 1.4 multiply_convert_fusion.7
  222.0 2.0 fusion.108
  225.5 2.6 convolution_convert_fusion.4
  228.1 1.9 copy.82
  230.0 3.3 convolution_convert_fusion.1
  233.4 1.6 multiply_reduce_fusion.1
  235.0 1.8 exponential_reduce_fusion
  237.3 1.5 convolution_convert_fusion.2
  238.9 3.2 multiply_convert_fusion.6
  244.9 8.3 %fusion.103 = (f32[200]{0:T(256)S(1)}, f32[200,3072]{1,0:T(8,128)S(1)}, f32[200,3072]{1,0:T(8,128)S(1)}, f32[200,3072]{1,0:T(8,128)S(1)}) fusion(bf16[2,768,3072]{2,1,0:T(8,128)(2,1)} %all-gather.9.cloned.1.call-done, f32[1,200,768]{2,1,0:T(8,128)} %copy-done.20, f32[768]{0:T(1024)S(1)} %copy-done.63, f32[200]{0:T(256)S(1)} %fusion.72, ...), kind=kOutput, calls=%fused_computation.231 | convolution fusion | flops 984268608 | bytes 12711264 | tf_op jit(solution)/shard_map/dot_general | solution.py:46
  253.3 1.5 multiply_reduce_fusion.4
  254.8 1.6 multiply_reduce_fusion.2
  256.4 2.0 add_convert_fusion
  258.4 2.4 fusion.49
  262.6 2.1 fusion.35
  264.8 4.1 multiply_reduce_fusion
  268.9 2.1 multiply_convert_fusion
  271.0 1.6 fusion.24
  273.0 2.7 fusion.51
  277.5 1.8 fusion.31
  286.3 3.9 pad_maximum_fusion.1
  293.0 3.4 multiply_convert_fusion.1
  296.4 6.2 convolution_convert_fusion
  302.7 1.6 convolution_bitcast_fusion.3
  304.3 1.6 convolution_bitcast_fusion.4
  305.9 4.0 pad_maximum_fusion.2
  310.2 3.3 convolution_bitcast_fusion.1
  313.6 1.6 convolution_bitcast_fusion
  315.1 7.3 pad_maximum_fusion
  322.5 2.5 copy.100
  330.1 2.1 fusion.30
  332.2 1.9 convolution_add_fusion.2
  334.2 2.1 fusion.48
  338.6 2.2 pad.9.clone
  340.8 6.7 reshape.933
  347.6 3.1 fusion.34
  350.7 2.7 fusion.110
  356.2 2.6 pad_convert_fusion
  358.7 7.9 reshape.939
  366.6 3.7 reduce_sum.426
  371.7 1.4 reverse.1
  373.1 1.3 stack.96
  374.5 1.4 multiply_reduce_fusion.6
  375.9 1.6 multiply_reduce_fusion.7
  378.9 48.3 %all-reduce.6 = (f32[2,768]{1,0:T(2,128)S(1)}, f32[3072]{0:T(1024)S(1)}, f32[5,768]{1,0:T(8,128)S(1)}, f32[512,12]{1,0:T(8,128)}, f32[2,12]{1,0:T(2,128)}) all-reduce(f32[2,768]{1,0:T(2,128)S(1)} %pad_maximum_fusion.3, f32[3072]{0:T(1024)} %get-tuple-element.12, ...), channel_id=1, replica_groups=mesh['wide'=16,'narrow'=2] {'wide','narrow'}, use_global_device_ids=true, to_apply=%region_36.37 | all-reduce | flops 14616 | bytes 116928 | tf_op jit(solution)/shard_map/psum | solution.py:317
  430.5 2.2 add_add_fusion.6
  432.7 4.0 fusion.13
  436.7 4.9 fusion.29
  441.6 129.6 %reduce-scatter.6.cloned.1.call-done = f32[24,4,768]{2,0,1:T(8,128)} async-done(((f32[768,4,768]{2,0,1:T(8,128)}), f32[24,4,768]{2,0,1:T(8,128)}) %reduce-scatter.6.cloned.1.call-update) | async-done | bytes 294928 | tf_op jit(solution)/shard_map/reduce_scatter | solution.py:252
  571.1 210.9 %reduce-scatter.8.cloned.1.call-done = f32[24,2,3072]{2,0,1:T(8,128)} async-done(((f32[768,2,3072]{2,0,1:T(8,128)}), f32[24,2,3072]{2,0,1:T(8,128)}) %reduce-scatter.8.cloned.1.call-update) | async-done | bytes 589840 | tf_op jit(solution)/shard_map/reduce_scatter | solution.py:220
  (340 shorter events, 48.7 us)
Async XLA Ops:
  7.2 203.4 %all-gather.5.cloned.1.call-start = ((), (), s32[]{:S(2)}) async-start(), calls=%async_computation.3 | async-start | bytes 4866048 | tf_op jit(solution)/shard_map/all_gather | solution.py:144
  7.9 217.5 %all-gather.7.cloned.1.call-start = ((), (), s32[]{:S(2)}) async-start(), calls=%async_computation.4 | async-start | bytes 4866048 | tf_op jit(solution)/shard_map/all_gather | solution.py:167
  8.7 236.2 %all-gather.9.cloned.1.call-start = ((), (), s32[]{:S(2)}) async-start(), calls=%async_computation.5 | async-start | bytes 9732096 | tf_op jit(solution)/shard_map/all_gather | solution.py:192
  9.4 432.2 %reduce-scatter.4.cloned.1.call-start = ((), (), s32[]{:S(2)}) async-start(), calls=%async_computation.6 | async-start | bytes 9732096 | tf_op jit(solution)/shard_map/reduce_scatter | solution.py:299
  164.4 3.4 copy-start.9
  164.4 44.0 %copy-start.4 = (bf16[1,200,768]{2,1,0:T(8,128)(2,1)S(1)}, bf16[1,200,768]{2,1,0:T(8,128)(2,1)}, u32[]{:S(2)}) copy-start(bf16[1,200,768]{2,1,0:T(8,128)(2,1)} %param.14) | copy-start | bytes 921604
  208.5 6.9 copy-start.67
  208.7 5.7 copy-start.95
  209.3 6.1 copy-start.71
  212.5 4.8 copy-start.45
  222.0 3.4 copy-start.75
  224.8 5.1 copy-start.76
  224.8 5.1 copy-start.80
  224.8 5.1 copy-start.102
  224.8 5.1 copy-start.104
  230.0 6.8 slice-start.3
  233.3 3.5 slice-start.4
  235.0 3.9 copy-start
  237.3 31.6 %copy-start.58 = (f32[12,200]{1,0:T(8,128)}, f32[12,200]{1,0:T(8,128)S(1)}, u32[]{:S(2)}) copy-start(f32[12,200]{1,0:T(8,128)S(1)} %log_add_fusion) | copy-start | bytes 28804
  243.8 17.1 %copy-start.84 = (f32[200]{0:T(256)}, f32[200]{0:T(256)S(1)}, u32[]{:S(2)}) copy-start(f32[200]{0:T(256)S(1)} %broadcast_multiply_fusion.2) | copy-start | bytes 2404
  244.8 16.0 %copy-start.91 = (f32[200]{0:T(256)}, f32[200]{0:T(256)S(1)}, u32[]{:S(2)}) copy-start(f32[200]{0:T(256)S(1)} %fusion.72) | copy-start | bytes 2404
  244.8 8.4 %copy-start.33 = (bf16[1,200,768]{2,1,0:T(8,128)(2,1)S(1)}, bf16[1,200,768]{2,1,0:T(8,128)(2,1)}, u32[]{:S(2)}) copy-start(bf16[1,200,768]{2,1,0:T(8,128)(2,1)} %param.17) | copy-start | bytes 921604
  244.9 8.4 %copy-start.60 = (f32[3072]{0:T(1024)S(1)}, f32[3072]{0:T(1024)}, u32[]{:S(2)}) copy-start(f32[3072]{0:T(1024)} %convert_element_type.192) | copy-start | bytes 36868
  244.9 8.4 %copy-start.107 = (bf16[2,768,3072]{2,1,0:T(8,128)(2,1)S(1)}, bf16[2,768,3072]{2,1,0:T(8,128)(2,1)}, u32[]{:S(2)}) copy-start(bf16[2,768,3072]{2,1,0:T(8,128)(2,1)} %all-gather.9.cloned.1.call-done) | copy-start | bytes 28311556
  258.4 6.3 slice-start
  258.4 6.3 slice-start.1
  260.8 3.9 slice-start.2
  262.6 6.2 copy-start.26
  264.7 4.2 copy-start.6
  280.6 3.7 copy-start.40
  290.3 280.9 %reduce-scatter.6.cloned.1.call-start = ((), (), s32[]{:S(2)}) async-start(), calls=%async_computation.7 | async-start | bytes 9732096 | tf_op jit(solution)/shard_map/reduce_scatter | solution.py:252
  293.0 3.4 copy-start.59
  293.0 3.4 copy-start.100
  296.4 8.0 %copy-start.55 = (bf16[12,64,896]{2,1,0:T(8,128)(2,1)}, bf16[12,64,896]{2,1,0:T(8,128)(2,1)S(1)}, u32[]{:S(2)}) copy-start(bf16[12,64,896]{2,1,0:T(8,128)(2,1)S(1)} %multiply_convert_fusion.1) | copy-start | bytes 4128772
  296.4 6.3 copy-start.11
  296.4 6.3 copy-start.77
  296.4 6.3 copy-start.81
  296.4 6.3 copy-start.103
  296.4 6.3 copy-start.105
  309.9 3.6 copy-start.3
  309.9 472.1 %reduce-scatter.8.cloned.1.call-start = ((), (), s32[]{:S(2)}) async-start(), calls=%async_computation.8 | async-start | bytes 19464192 | tf_op jit(solution)/shard_map/reduce_scatter | solution.py:220
  310.1 3.4 copy-start.34
  310.1 3.4 copy-start.61
  310.2 3.4 copy-start.86
  310.2 3.4 copy-start.89
  325.0 7.2 copy-start.43
  330.1 4.0 copy-start.41
  330.1 4.0 copy-start.69
  332.2 4.0 copy-start.96
  332.2 4.8 copy-start.73
  334.1 4.5 copy-start.32
  375.9 54.5 %copy-start.106 = (f32[200]{0:T(256)S(1)}, f32[200]{0:T(256)}, u32[]{:S(2)}) copy-start(f32[200]{0:T(256)} %get-tuple-element.27) | copy-start | bytes 2404
  375.9 54.5 %copy-start.24 = (f32[1,200,768]{2,1,0:T(8,128)S(1)}, f32[1,200,768]{2,1,0:T(8,128)}, u32[]{:S(2)}) copy-start(f32[1,200,768]{2,1,0:T(8,128)} %copy-done.23) | copy-start | bytes 1843204
  375.9 54.5 %copy-start.70 = (f32[200]{0:T(256)S(1)}, f32[200]{0:T(256)}, u32[]{:S(2)}) copy-start(f32[200]{0:T(256)} %copy-done.67) | copy-start | bytes 2404
  375.9 54.5 %copy-start.74 = (f32[200]{0:T(256)S(1)}, f32[200]{0:T(256)}, u32[]{:S(2)}) copy-start(f32[200]{0:T(256)} %copy-done.71) | copy-start | bytes 2404
  375.9 54.5 %copy-start.98 = (f32[200]{0:T(256)S(1)}, f32[200]{0:T(256)}, u32[]{:S(2)}) copy-start(f32[200]{0:T(256)} %copy-done.97) | copy-start | bytes 2404
  375.9 56.7 %copy-start.79 = (f32[768]{0:T(1024)S(1)}, f32[768]{0:T(1024)}, u32[]{:S(2)}) copy-start(f32[768]{0:T(1024)} %get-tuple-element.62) | copy-start | bytes 9220
  375.9 56.7 %copy-start.83 = (f32[768]{0:T(1024)S(1)}, f32[768]{0:T(1024)}, u32[]{:S(2)}) copy-start(f32[768]{0:T(1024)} %get-tuple-element.65) | copy-start | bytes 9220
  375.9 56.7 %copy-start.92 = (f32[768]{0:T(1024)S(1)}, f32[768]{0:T(1024)}, u32[]{:S(2)}) copy-start(f32[768]{0:T(1024)} %get-tuple-element.61) | copy-start | bytes 9220
  427.2 5.4 copy-start.13
  432.6 4.0 copy-start.22
  432.6 4.0 copy-start.62
  432.6 4.0 copy-start.87
  432.7 4.0 copy-start.90
  (55 other events, 119.0 us)
Sparse Core Ops, SparseCore 0:
  10.9 66.7 all-gather.4
  80.7 61.9 all-gather.6
  145.6 81.8 all-gather.8
  290.4 139.1 reduce-scatter.3
  435.9 135.1 reduce-scatter.5
  578.0 203.9 reduce-scatter.7
where the time goes:
time: 798 us; the launch traced here: 789 us
  waiting for transfers between devices  343 us (43%)
  blocking collectives  209 us (26%)
  matrix products  91.6 us (11%)
  local copies, waits for them, and re-layouts  78.9 us (10%)
  other arithmetic  50.1 us (6%)
  between operations  16.6 us (2%)
    reduce_scatter x1, waiting for transfers between devices, body(): lax.psum_scatter(jnp.stack([grad_in, grad_out], axis=1), ('wide', 'narrow...  211 us
    reduce_scatter x1, waiting for transfers between devices, body(): lax.psum_scatter(jnp.stack([weight_grad(normed_two, grad_cross_query), we...  130 us
    psum x1, blocking collectives, body(): lax.psum((jnp.stack([scale_part, bias_part]), jnp.stack([self_head, cross...  48.3 us
    unnamed x1, blocking collectives  42.3 us
    all_gather x1, blocking collectives, body(): lax.all_gather(norm_gains, ('wide', 'narrow'), axis=1, tiled=True)  40.9 us
    psum x1, blocking collectives, body(): lax.psum((jnp.sum(memory_values, axis=(0, 1)), jnp.sum(memory_values * me...  39.5 us
    all_gather x1, blocking collectives, body(): lax.all_gather(rel_table, ('wide', 'narrow'), axis=0, tiled=True)  37.8 us
    dot_general x9, matrix products, product(): return jnp.dot(left_side, right_side, preferred_element_type=jnp.float32)  23.7 us
  transfers between devices with their start and end apart: 6, of which 2 were waited for; matrix products, arithmetic and copies ran while one was open for 21% of the time, Pallas kernels for 0%

commit v1 on v0

--- a/solution.py
+++ b/solution.py
@@ -9,6 +9,28 @@
 EPSILON = 1e-05
 NEGATIVE = -1000000000.0
 HIGHEST = lax.Precision.HIGHEST
+
+
+def laid_out(blocks, dim):
+    blocks = jnp.moveaxis(blocks, 0, dim)
+    shape = blocks.shape
+    return blocks.reshape(*shape[:dim], shape[dim] * shape[dim + 1], *shape[dim + 2 :])
+
+
+def collected_by_bits(shard, axis):
+    length = lax.axis_size(axis)
+    blocks = shard[None]
+    for level in range(length.bit_length() - 1):
+        apart = 1 << level
+        other = lax.ppermute(blocks, axis, [(i, i ^ apart) for i in range(length)])
+        both = jnp.stack([blocks, other])
+        upper = lax.axis_index(axis) >> level & 1
+        blocks = jnp.where(upper == 0, both, both[::-1]).reshape(-1, *shard.shape)
+    return blocks
+
+
+def gather_by_bits(shard, axis, dim):
+    return laid_out(collected_by_bits(shard, axis), dim)
 
 
 def bucket_select(length, buckets):
@@ -143,7 +165,7 @@
     self_full, gains_full, table_full = (
         lax.all_gather(self_proj, ("wide", "narrow"), axis=1, tiled=True),
         lax.all_gather(norm_gains, ("wide", "narrow"), axis=1, tiled=True),
-        lax.all_gather(rel_table, ("wide", "narrow"), axis=0, tiled=True),
+        gather_by_bits(rel_table, ("wide", "narrow"), 0),
     )
     norm_scale = gains_full.astype(jnp.float32)
     select = jnp.asarray(bucket_select(length, table_full.shape[0]))

time: 798 us -> 773 us (0.969)
  blocking collectives: 209 us -> 171 us
  waiting for transfers between devices: 343 us -> 353 us
    all_gather x1 -> x0, blocking collectives: 37.8 us -> none  [body(): lax.all_gather(rel_table, ('wide', 'narrow'), axis=0, tiled=True)]
    unnamed x237 -> x239, local copies, waits for them, and re-layouts: 18.4 us -> 17.4 us
  transfers between devices with their start and end apart: 6 -> 11, of which waited for: 2 -> 6; matrix products, arithmetic and copies ran while one was open for 21% -> 22% of each run, Pallas kernels for 0% -> 0%
where the time goes in v1:
time: 773 us; the launch traced here: 768 us
  waiting for transfers between devices  353 us (46%)
  blocking collectives  171 us (22%)
  matrix products  90.6 us (12%)
  local copies, waits for them, and re-layouts  76.9 us (10%)
  other arithmetic  53.5 us (7%)
  between operations  16.9 us (2%)
    reduce_scatter x1, waiting for transfers between devices, body(): lax.psum_scatter(jnp.stack([grad_in, grad_out], axis=1), ('wide', 'narrow...  211 us
    reduce_scatter x1, waiting for transfers between devices, body(): lax.psum_scatter(jnp.stack([weight_grad(normed_two, grad_cross_query), we...  128 us
    psum x1, blocking collectives, body(): lax.psum((jnp.stack([scale_part, bias_part]), jnp.stack([self_head, cross...  46.5 us
    unnamed x1, blocking collectives  41.8 us
    all_gather x1, blocking collectives, body(): lax.all_gather(norm_gains, ('wide', 'narrow'), axis=1, tiled=True)  41.6 us
    psum x1, blocking collectives, body(): lax.psum((jnp.sum(memory_values, axis=(0, 1)), jnp.sum(memory_values * me...  40.6 us
    dot_general x9, matrix products, product(): return jnp.dot(left_side, right_side, preferred_element_type=jnp.float32)  24 us
    dot_general x8, matrix products, back_product(): jnp.einsum('ble,de->bld', upstream, weight, preferred_element_type=jnp.fl...  18.3 us
  transfers between devices with their start and end apart: 11, of which 6 were waited for; matrix products, arithmetic and copies ran while one was open for 22% of the time, Pallas kernels for 0%

profile of v1, /device:TPU:0, one launch (start us, length us, event | category | flops | bytes accessed | tf_op | source)
XLA Modules:
  0.0 768.1 jit_solution(6523100849593663572)
XLA Ops:
  13.9 41.8 %all-reduce.8 = (bf16[768]{0:T(1024)(128)(2,1)S(1)}, bf16[768]{0:T(1024)(128)(2,1)S(1)}, bf16[3072]{0:T(1024)(128)(2,1)S(1)}) all-reduce(bf16[768]{0:T(1024)(128)(2,1)S(1)} %dynamic-update-slice.1, bf16[768]{0:T(1024)(128)(2,1)S(1)} %dynamic-update-slice, ...), channel_id=1, replica_groups=mesh['wide'=16,'narrow'=2] {'wide','narrow'}, use_global_device_ids=true, to_apply=%add.4 | all-reduce | flops 4608 | bytes 18432
  55.7 1.7 convert_reduce_fusion
  57.4 40.6 %all-reduce.7 = (f32[768]{0:T(1024)S(1)}, f32[768]{0:T(1024)S(1)}) all-reduce(f32[768]{0:T(1024)S(1)} %get-tuple-element.19, f32[768]{0:T(1024)S(1)} %get-tuple-element.18), channel_id=1, replica_groups=mesh['wide'=16,'narrow'=2] {'wide','narrow'}, use_global_device_ids=true, to_apply=%region_9.10 | all-reduce | flops 1536 | bytes 12288 | tf_op jit(solution)/shard_map/psum | solution.py:194
  101.7 2.3 collective-permute-start.1
  105.7 2.1 collective-permute-start.2
  107.8 1.7 collective-permute-done.2
  110.4 41.6 %all-gather = bf16[32,24,5]{1,2,0:T(8,128)(2,1)S(1)} all-gather(bf16[1,24,5]{1,2,0:T(8,128)(2,1)S(1)} %bitcast.378), channel_id=1, replica_groups=mesh['wide'=16,'narrow'=2] {'wide','narrow'}, dimensions={0}, use_global_device_ids=true | all-gather | bytes 7920 | tf_op jit(solution)/shard_map/all_gather | solution.py:167
  154.9 4.8 collective-permute-done.4
  160.3 2.9 tile.4
  163.2 7.0 tile.10
  170.2 5.3 slice.107
  175.5 7.2 reshape.929
  182.7 2.8 slice.108
  185.4 2.3 copy.99
  187.8 1.8 convolution_convert_fusion.6
  189.7 1.9 convolution_convert_fusion.5
  192.5 1.8 convolution_convert_fusion.7
  194.5 2.6 fusion.109
  199.2 2.0 fusion.110
  202.7 2.5 convolution_convert_fusion.4
  205.1 1.9 copy.82
  207.1 3.3 convolution_convert_fusion.1
  210.4 1.6 multiply_reduce_fusion.1
  212.0 1.8 exponential_reduce_fusion
  214.4 1.5 convolution_convert_fusion.2
  215.9 3.0 multiply_convert_fusion.6
  221.7 4.5 all-gather.9.cloned.1.call-done
  226.2 8.8 %fusion.105 = (f32[200]{0:T(256)S(1)}, f32[200,3072]{1,0:T(8,128)S(1)}, f32[200,3072]{1,0:T(8,128)S(1)}, f32[200,3072]{1,0:T(8,128)S(1)}) fusion(bf16[2,768,3072]{2,1,0:T(8,128)(2,1)} %all-gather.9.cloned.1.call-done, f32[1,200,768]{2,1,0:T(8,128)} %copy-done.19, f32[768]{0:T(1024)S(1)} %copy-done.63, f32[200]{0:T(256)S(1)} %fusion.74, ...), kind=kOutput, calls=%fused_computation.242 | convolution fusion | flops 984268608 | bytes 12711264 | tf_op jit(solution)/shard_map/dot_general | solution.py:68
  236.5 1.6 multiply_reduce_fusion.2
  238.1 2.0 add_convert_fusion
  240.1 2.4 fusion.49
  244.4 2.1 fusion.35
  246.5 3.7 multiply_reduce_fusion
  250.2 2.3 multiply_convert_fusion
  252.5 1.6 fusion.24
  254.5 2.7 fusion.51
  259.0 1.8 fusion.31
  267.8 4.0 pad_maximum_fusion.1
  274.5 3.6 multiply_convert_fusion.1
  278.2 6.3 convolution_convert_fusion
  284.5 1.6 convolution_bitcast_fusion.3
  286.1 1.6 convolution_bitcast_fusion.4
  287.7 4.0 pad_maximum_fusion.2
  292.1 3.4 convolution_bitcast_fusion.1
  295.5 1.6 convolution_bitcast_fusion
  297.1 7.3 pad_maximum_fusion
  304.4 2.5 copy.100
  312.0 2.0 fusion.30
  314.1 1.8 convolution_add_fusion.2
  316.0 2.0 fusion.48
  320.4 2.2 pad.9.clone
  322.6 6.9 reshape.949
  329.6 3.1 fusion.34
  332.7 2.7 fusion.112
  338.2 2.5 pad_convert_fusion
  340.8 8.0 %reshape.955 = f32[12,200,400]{2,1,0:T(8,128)} reshape(f32[12,80000]{1,0:T(8,128)} %pad_convert_fusion) | data formatting | bytes 7680000 | tf_op jit(solution)/shard_map/transpose(jvp())/reshape | solution.py:51
  348.8 3.7 reduce_sum.426
  358.1 1.7 multiply_reduce_fusion.7
  361.1 46.5 %all-reduce.6 = (f32[2,768]{1,0:T(2,128)S(1)}, f32[3072]{0:T(1024)S(1)}, f32[5,768]{1,0:T(8,128)S(1)}, f32[512,12]{1,0:T(8,128)}, f32[2,12]{1,0:T(2,128)}) all-reduce(f32[2,768]{1,0:T(2,128)S(1)} %pad_maximum_fusion.8, f32[3072]{0:T(1024)} %get-tuple-element.12, ...), channel_id=1, replica_groups=mesh['wide'=16,'narrow'=2] {'wide','narrow'}, use_global_device_ids=true, to_apply=%region_36.37 | all-reduce | flops 14616 | bytes 116928 | tf_op jit(solution)/shard_map/psum | solution.py:339
  410.9 2.2 add_add_fusion.6
  413.1 4.0 fusion.13
  417.1 5.0 fusion.29
  422.1 127.9 %reduce-scatter.6.cloned.1.call-done = f32[24,4,768]{2,0,1:T(8,128)} async-done(((f32[768,4,768]{2,0,1:T(8,128)}), f32[24,4,768]{2,0,1:T(8,128)}) %reduce-scatter.6.cloned.1.call-update) | async-done | bytes 294928 | tf_op jit(solution)/shard_map/reduce_scatter | solution.py:274
  550.0 210.8 %reduce-scatter.8.cloned.1.call-done = f32[24,2,3072]{2,0,1:T(8,128)} async-done(((f32[768,2,3072]{2,0,1:T(8,128)}), f32[24,2,3072]{2,0,1:T(8,128)}) %reduce-scatter.8.cloned.1.call-update) | async-done | bytes 589840 | tf_op jit(solution)/shard_map/reduce_scatter | solution.py:242
  (361 shorter events, 59.1 us)
Async XLA Ops:
  7.2 152.6 %copy-start.47 = (f32[512,200]{1,0:T(8,128)S(1)}, f32[512,200]{1,0:T(8,128)}, u32[]{:S(2)}) copy-start(f32[512,200]{1,0:T(8,128)} %constant.148.clone) | copy-start | bytes 1228804
  7.2 96.9 %copy-start.4 = (bf16[1,200,768]{2,1,0:T(8,128)(2,1)S(1)}, bf16[1,200,768]{2,1,0:T(8,128)(2,1)}, u32[]{:S(2)}) copy-start(bf16[1,200,768]{2,1,0:T(8,128)(2,1)} %param.14) | copy-start | bytes 921604
  7.2 103.2 %copy-start.107 = (bf16[5,24]{1,0:T(8,128)(2,1)S(1)}, bf16[5,24]{1,0:T(8,128)(2,1)}, u32[]{:S(2)}) copy-start(bf16[5,24]{1,0:T(8,128)(2,1)} %param.22) | copy-start | bytes 724
  7.2 180.5 %all-gather.5.cloned.1.call-start = ((), (), s32[]{:S(2)}) async-start(), calls=%async_computation.3 | async-start | bytes 4866048 | tf_op jit(solution)/shard_map/all_gather | solution.py:166
  7.9 194.7 %all-gather.7.cloned.1.call-start = ((), (), s32[]{:S(2)}) async-start(), calls=%async_computation.4 | async-start | bytes 4866048 | tf_op jit(solution)/shard_map/all_gather | solution.py:189
  8.7 217.5 %all-gather.9.cloned.1.call-start = ((), (), s32[]{:S(2)}) async-start(), calls=%async_computation.5 | async-start | bytes 9732096 | tf_op jit(solution)/shard_map/all_gather | solution.py:214
  9.4 412.7 %reduce-scatter.4.cloned.1.call-start = ((), (), s32[]{:S(2)}) async-start(), calls=%async_computation.6 | async-start | bytes 9732096 | tf_op jit(solution)/shard_map/reduce_scatter | solution.py:321
  9.5 91.5 %collective-permute-start = (bf16[1,16,12]{2,1,0:T(8,128)(2,1)}, bf16[1,16,12]{2,1,0:T(8,128)(2,1)S(1)}, u32[]{:S(2)}, u32[]{:S(2)}) collective-permute-start(bf16[1,16,12]{2,1,0:T(8,128)(2,1)} %bitcast.373), channel_id=1, source_target_pairs={{0,1},{1,0},{2,3},{3,2},{4,5},{5,4},{6,7},{7,6},{8,9},{9,8},{10,11... | collective-permute-start | bytes 1160 | tf_op jit(solution)/shard_map/ppermute | solution.py:25
  99.7 92.8 %copy-start.67 = (f32[200]{0:T(256)}, f32[200]{0:T(256)S(1)}, u32[]{:S(2)}) copy-start(f32[200]{0:T(256)S(1)} %broadcast_multiply_fusion.6) | copy-start | bytes 2404
  101.7 4.0 collective-permute-start.1
  104.3 47.8 %copy-start.95 = (f32[200]{0:T(256)}, f32[200]{0:T(256)S(1)}, u32[]{:S(2)}) copy-start(f32[200]{0:T(256)S(1)} %fusion.47) | copy-start | bytes 2404
  105.7 3.8 collective-permute-start.2
  107.8 84.7 %copy-start.71 = (f32[200]{0:T(256)}, f32[200]{0:T(256)S(1)}, u32[]{:S(2)}) copy-start(f32[200]{0:T(256)S(1)} %fusion.70) | copy-start | bytes 2404
  109.6 42.8 %collective-permute-start.3 = (bf16[8,16,12]{2,1,0:T(8,128)(2,1)S(1)}, bf16[8,16,12]{2,1,0:T(8,128)(2,1)S(1)}, u32[]{:S(2)}, u32[]{:S(2)}) collective-permute-start(bf16[8,16,12]{2,1,0:T(8,128)(2,1)S(1)} %bitcast.362), channel_id=1, source_target_pairs={{0,8},{1,9},{2,10},{3,11},{4,12},{5,13},{6,14},{7,15},{8,0},{9,1},... | collective-permute-start | bytes 9224 | tf_op jit(solution)/shard_map/ppermute | solution.py:25
  152.4 7.3 collective-permute-start.4
  189.7 4.8 copy-start.44
  202.1 5.0 copy-start.76
  202.1 5.0 copy-start.80
  202.1 5.0 copy-start.102
  202.1 5.0 copy-start.104
  207.1 6.8 slice-start.3
  212.0 3.9 copy-start
  214.4 35.8 %copy-start.58 = (f32[12,200]{1,0:T(8,128)}, f32[12,200]{1,0:T(8,128)S(1)}, u32[]{:S(2)}) copy-start(f32[12,200]{1,0:T(8,128)S(1)} %log_add_fusion) | copy-start | bytes 28804
  219.0 7.2 copy-start.63
  220.6 22.0 %copy-start.84 = (f32[200]{0:T(256)}, f32[200]{0:T(256)S(1)}, u32[]{:S(2)}) copy-start(f32[200]{0:T(256)S(1)} %broadcast_multiply_fusion.2) | copy-start | bytes 2404
  221.6 20.9 %copy-start.91 = (f32[200]{0:T(256)}, f32[200]{0:T(256)S(1)}, u32[]{:S(2)}) copy-start(f32[200]{0:T(256)S(1)} %fusion.74) | copy-start | bytes 2404
  226.2 8.8 %copy-start.32 = (bf16[1,200,768]{2,1,0:T(8,128)(2,1)S(1)}, bf16[1,200,768]{2,1,0:T(8,128)(2,1)}, u32[]{:S(2)}) copy-start(bf16[1,200,768]{2,1,0:T(8,128)(2,1)} %param.17) | copy-start | bytes 921604
  226.2 8.9 %copy-start.60 = (f32[3072]{0:T(1024)S(1)}, f32[3072]{0:T(1024)}, u32[]{:S(2)}) copy-start(f32[3072]{0:T(1024)} %convert_element_type.192) | copy-start | bytes 36868
  226.2 8.9 %copy-start.108 = (bf16[2,768,3072]{2,1,0:T(8,128)(2,1)S(1)}, bf16[2,768,3072]{2,1,0:T(8,128)(2,1)}, u32[]{:S(2)}) copy-start(bf16[2,768,3072]{2,1,0:T(8,128)(2,1)} %all-gather.9.cloned.1.call-done) | copy-start | bytes 28311556
  240.1 6.3 slice-start
  240.1 6.3 slice-start.1
  242.6 3.9 slice-start.2
  244.4 5.8 copy-start.25
  246.4 3.8 copy-start.6
  262.1 3.7 copy-start.39
  271.8 278.2 %reduce-scatter.6.cloned.1.call-start = ((), (), s32[]{:S(2)}) async-start(), calls=%async_computation.7 | async-start | bytes 9732096 | tf_op jit(solution)/shard_map/reduce_scatter | solution.py:274
  274.5 3.6 copy-start.100
  278.1 8.0 %copy-start.55 = (bf16[12,64,896]{2,1,0:T(8,128)(2,1)}, bf16[12,64,896]{2,1,0:T(8,128)(2,1)S(1)}, u32[]{:S(2)}) copy-start(bf16[12,64,896]{2,1,0:T(8,128)(2,1)S(1)} %multiply_convert_fusion.1) | copy-start | bytes 4128772
  278.1 6.3 copy-start.10
  278.2 6.3 copy-start.77
  278.2 6.3 copy-start.81
  278.2 6.3 copy-start.103
  278.2 6.3 copy-start.105
  291.8 3.7 copy-start.3
  291.8 469.1 %reduce-scatter.8.cloned.1.call-start = ((), (), s32[]{:S(2)}) async-start(), calls=%async_computation.8 | async-start | bytes 19464192 | tf_op jit(solution)/shard_map/reduce_scatter | solution.py:242
  306.9 7.2 copy-start.42
  312.0 3.9 copy-start.40
  312.0 3.9 copy-start.69
  314.1 3.9 copy-start.96
  314.1 4.8 copy-start.73
  315.9 4.5 copy-start.31
  358.0 52.8 %copy-start.106 = (f32[200]{0:T(256)S(1)}, f32[200]{0:T(256)}, u32[]{:S(2)}) copy-start(f32[200]{0:T(256)} %get-tuple-element.27) | copy-start | bytes 2404
  358.0 52.8 %copy-start.23 = (f32[1,200,768]{2,1,0:T(8,128)S(1)}, f32[1,200,768]{2,1,0:T(8,128)}, u32[]{:S(2)}) copy-start(f32[1,200,768]{2,1,0:T(8,128)} %copy-done.22) | copy-start | bytes 1843204
  358.0 52.8 %copy-start.70 = (f32[200]{0:T(256)S(1)}, f32[200]{0:T(256)}, u32[]{:S(2)}) copy-start(f32[200]{0:T(256)} %copy-done.67) | copy-start | bytes 2404
  358.0 52.8 %copy-start.74 = (f32[200]{0:T(256)S(1)}, f32[200]{0:T(256)}, u32[]{:S(2)}) copy-start(f32[200]{0:T(256)} %copy-done.71) | copy-start | bytes 2404
  358.0 52.8 %copy-start.98 = (f32[200]{0:T(256)S(1)}, f32[200]{0:T(256)}, u32[]{:S(2)}) copy-start(f32[200]{0:T(256)} %copy-done.97) | copy-start | bytes 2404
  358.0 55.0 %copy-start.79 = (f32[768]{0:T(1024)S(1)}, f32[768]{0:T(1024)}, u32[]{:S(2)}) copy-start(f32[768]{0:T(1024)} %get-tuple-element.62) | copy-start | bytes 9220
  358.0 55.0 %copy-start.83 = (f32[768]{0:T(1024)S(1)}, f32[768]{0:T(1024)}, u32[]{:S(2)}) copy-start(f32[768]{0:T(1024)} %get-tuple-element.67) | copy-start | bytes 9220
  358.1 55.0 %copy-start.92 = (f32[768]{0:T(1024)S(1)}, f32[768]{0:T(1024)}, u32[]{:S(2)}) copy-start(f32[768]{0:T(1024)} %get-tuple-element.61) | copy-start | bytes 9220
  407.7 5.4 copy-start.12
  413.1 4.0 copy-start.21
  413.1 4.0 copy-start.62
  413.1 4.0 copy-start.87
  413.1 4.0 copy-start.90
  (61 other events, 140.8 us)
Sparse Core Ops, SparseCore 0:
  11.0 66.9 all-gather.4
  80.9 62.2 all-gather.6
  146.2 79.9 all-gather.8
  272.0 136.5 reduce-scatter.3
  414.9 135.1 reduce-scatter.5
  556.9 203.9 reduce-scatter.7
